TPU v7x, 32 devices: a whole 2x2x4 slice. The times are simulated.
32 devices in a mesh: dp: 8 (over z, x), mp: 4 (over y, core).
Axes of the slice: x: 2, y: 2, z: 4, core: 2. Of those that a mesh axis runs over, the one named last changes fastest.
Arguments:
- gradients: bfloat16 [8, 3584, 14336], P(None, 'dp', 'mp'), may hold values from -60 to 60
- column_slot: int32 [8, 16], replicated, may hold values from 0 to 31, as said below
- left_roots: bfloat16 [32, 4, 4, 896, 896], P('dp', 'mp'), may hold values from -1 to 5
- right_roots: bfloat16 [32, 4, 4, 896, 896], P('dp', 'mp'), may hold values from -1 to 5
Outputs:
- update: bfloat16 [8, 3584, 14336], P(None, 'dp', 'mp')
- clip_scale: float32 [], replicated
Inputs may be any that keep to these rules, and one draw needn't show every extreme that they name: `column_slot`: block column c belongs to group c // 4; over all matrices, the entries of one group's block columns are a permutation of 0 to 31.
All inputs are finite; a program needn't handle non-finite values.
Results may differ from a plain program's by a relative error of at most 0.0049.
Values may be sent and summed in bfloat16 or wider, within the bound.
A program may use at most 256 MiB of HBM per device.

v0:
```python
import jax
import jax.numpy as jnp
from jax import lax
from jax.sharding import PartitionSpec as P

D = 3584
FF = 14336
BLOCK = 896
MATRICES = 8


rms_limit = 0.25
epsilon = 1e-06


def body(gradients, column_slot, left_roots, right_roots):
    row_count = gradients.shape[1]
    local_cols = gradients.shape[2] // BLOCK
    slot_count = MATRICES * local_cols
    mp_index = lax.axis_index("mp")
    my_slots = lax.dynamic_slice_in_dim(column_slot, mp_index * local_cols, local_cols, 1).reshape(
        slot_count
    )
    columns = (
        gradients.reshape(MATRICES, row_count, local_cols, BLOCK)
        .transpose(0, 2, 1, 3)
        .reshape(slot_count, row_count, BLOCK)
    )
    send_order = jnp.argsort(my_slots)
    ordered = jnp.take(columns, send_order, axis=0)
    owned_cols = lax.all_to_all(ordered, "dp", split_axis=0, concat_axis=1, tiled=True)
    square_sum = lax.psum(jnp.sum(jnp.square(gradients.astype(jnp.float32))), ("dp", "mp"))
    clip_scale = jnp.minimum(
        jnp.float32(1.0), rms_limit / jnp.sqrt(square_sum / (MATRICES * D * FF) + epsilon)
    )
    owned_count = owned_cols.shape[0]
    owned_blocks = owned_cols.reshape(owned_count, D // BLOCK, BLOCK, BLOCK)
    left_root = left_roots[:, 0]
    right_root = right_roots[:, 0]
    first_product = jnp.einsum(
        "snab,snbc->snac", left_root, owned_blocks, preferred_element_type=jnp.float32
    )
    scaled = (clip_scale * first_product).astype(jnp.bfloat16)
    second_product = jnp.einsum(
        "snab,snbc->snac", scaled, right_root, preferred_element_type=jnp.float32
    )
    finished = second_product.astype(jnp.bfloat16).reshape(owned_count, D, BLOCK)
    returned = lax.all_to_all(finished, "dp", split_axis=1, concat_axis=0, tiled=True)
    restored = jnp.take(returned, my_slots, axis=0)
    update = (
        restored.reshape(MATRICES, local_cols, row_count, BLOCK)
        .transpose(0, 2, 1, 3)
        .reshape(MATRICES, row_count, local_cols * BLOCK)
    )
    return (update, clip_scale)


def solution(mesh):
    return jax.shard_map(
        body,
        mesh=mesh,
        in_specs=(
            P(None, "dp", "mp"),
            P(),
            P("dp", "mp", None, None, None),
            P("dp", "mp", None, None, None),
        ),
        out_specs=(P(None, "dp", "mp"), P()),
        check_vma=False,
    )
```

profile of v0, /device:TPU:0, one launch (start us, length us, event | category | flops | bytes accessed | tf_op | source)
XLA Modules:
  0.0 1468.3 jit_solution(521979596373554846)
XLA Ops:
  0.6 0.0 copy-start
  0.7 0.7 copy-done
  1.3 0.1 constant_dynamic-slice_fusion
  1.4 0.1 reshape.30
  1.5 0.0 copy-start.2
  1.5 1.6 sort.17
  3.1 0.0 copy-done.2
  3.1 17.6 %fusion.8 = (bf16[8,448,896]{2,1,0:T(8,128)(2,1)}, bf16[8,448,896]{2,1,0:T(8,128)(2,1)}, bf16[8,448,896]{2,1,0:T(8,128)(2,1)}, bf16[8,448,896]{2,1,0:T(8,128)(2,1)}) fusion(bf16[8,448,3584]{2,1,0:T(8,128)(2,1)} %param.6), kind=kLoop, calls=%fused_computation.18 | loop fusion | bytes 51380224 | tf_op jit(solution)/shard_map/slice
  20.8 18.6 %pad_maximum_fusion = bf16[8,1792,896]{2,1,0:T(8,128)(2,1)} fusion(bf16[8,448,896]{2,1,0:T(8,128)(2,1)} %get-tuple-element.7, bf16[8,448,896]{2,1,0:T(8,128)(2,1)} %get-tuple-element.8, bf16[8,448,896]{2,1,0:T(8,128)(2,1)} %get-tuple-element.6, bf16[8,448,896]{2,1,0:T(8,128)(2,1)} %get-tuple-element.5), kind=kLoop, calls=%fused_computation.4 | loop fusion | flops 102760448 | bytes 51380224 | tf_op jit(solution)/shard_map/concatenate
  39.4 18.9 %gather_fusion = bf16[32,448,896]{2,1,0:T(8,128)(2,1)} fusion(bf16[32,448,896]{2,1,0:T(8,128)(2,1)} %bitcast.34, s32[1024]{0:T(1024)S(1)} %pad_clamp_fusion.1), kind=kCustom, calls=%fused_computation.clone | custom fusion | bytes 51380352 | tf_op jit(solution)/shard_map/jit(_take)/gather | solution.py:30
  58.3 21.6 %broadcast_select_fusion.1 = bf16[32,448,896]{2,1,0:T(8,128)(2,1)} fusion(bf16[32,448,896]{2,1,0:T(8,128)(2,1)} %gather_fusion, pred[32]{0:T(512)(128)(4,1)S(1)} %compare_and_fusion.1), kind=kLoop, calls=%fused_computation.9 | loop fusion | flops 12845056 | bytes 51380256 | tf_op jit(solution)/shard_map/jit(_take)/select_n | solution.py:30
  79.8 7.3 all-to-all-start
  87.1 15.9 %multiply_reduce_fusion = f32[]{:T(128)} fusion(bf16[8,448,3584]{2,1,0:T(8,128)(2,1)} %param.6), kind=kLoop, calls=%fused_computation.3 | loop fusion | flops 38535168 | bytes 25690116 | tf_op jit(solution)/shard_map/reduce_sum | solution.py:32
  103.0 559.1 %psum.7 = f32[]{:T(128)} all-reduce(f32[]{:T(128)} %multiply_reduce_fusion), channel_id=1, replica_groups=mesh['dp'=8,'mp'=4] {'dp','mp'}, use_global_device_ids=true, to_apply=%region_1.2 | all-reduce | flops 1 | bytes 8 | tf_op jit(solution)/shard_map/psum | solution.py:32
  662.8 0.0 all-to-all-done
  662.8 21.0 %copy.11 = bf16[4,8,448,896]{3,2,1,0:T(8,128)(2,1)} copy(bf16[4,8,448,896]{3,2,0,1:T(8,128)(2,1)} %bitcast.2) | data formatting | bytes 51380224 | tf_op jit(solution)/shard_map/all_to_all | solution.py:31
  683.8 43.5 %multiply_convert_fusion.clone.4 = bf16[4,4,896,896]{3,2,1,0:T(8,128)(2,1)} fusion(bf16[4,4,896,896]{3,2,1,0:T(8,128)(2,1)} %bitcast.39, bf16[4,1,4,896,896]{4,3,2,1,0:T(8,128)(2,1)} %param.8, f32[]{:T(128)} %min_shard_map.3), kind=kOutput, calls=%fused_computation.2.clone.clone.clone.1 | convolution fusion | flops 23044030464 | bytes 77070336 | tf_op jit(solution)/shard_map/snab,snbc->snac/dot_general | solution.py:40
  727.3 43.5 %fusion.3 = bf16[4,4,896,896]{3,2,1,0:T(8,128)(2,1)} fusion(bf16[4,1,4,896,896]{4,3,2,1,0:T(8,128)(2,1)} %param.9, bf16[4,4,896,896]{3,2,1,0:T(8,128)(2,1)} %multiply_convert_fusion.clone.4), kind=kOutput, calls=%fused_computation.10 | convolution fusion | flops 23031185408 | bytes 77070336 | tf_op jit(solution)/shard_map/snab,snbc->snac/dot_general | solution.py:44
  770.8 56.9 %copy.14 = bf16[4,3584,896]{2,0,1:T(4,128)(2,1)} copy(bf16[4,3584,896]{2,1,0:T(8,128)(2,1)} %bitcast.40) | data formatting | bytes 51380224 | tf_op jit(solution)/shard_map/reshape | solution.py:47
  827.7 0.0 copy-start.3
  827.7 6.5 all-to-all-start.1
  834.2 0.0 copy-done.3
  834.2 553.4 %all-to-all-done.1 = bf16[4,3584,896]{2,0,1:T(4,128)(2,1)} async-done(((bf16[4,3584,896]{2,0,1:T(4,128)(2,1)}), bf16[4,3584,896]{2,0,1:T(4,128)(2,1)}, u32[]{:S(2)}, u32[]{:S(2)}) %all-to-all-start.1) | async-done | bytes 25690144 | tf_op jit(solution)/shard_map/all_to_all | solution.py:48
  1387.7 17.5 %copy.15 = bf16[4,3584,896]{2,1,0:T(8,128)(2,1)} copy(bf16[4,3584,896]{2,0,1:T(4,128)(2,1)} %all-to-all-done.1) | data formatting | bytes 51380224 | tf_op jit(solution)/shard_map/all_to_all | solution.py:48
  1405.2 21.0 %copy.16 = bf16[8,4,448,896]{3,2,1,0:T(8,128)(2,1)} copy(bf16[8,4,448,896]{3,2,0,1:T(8,128)(2,1)} %bitcast.37) | data formatting | bytes 51380224 | tf_op jit(solution)/shard_map/all_to_all | solution.py:48
  1426.2 19.2 %gather_fusion.1 = bf16[32,448,896]{2,1,0:T(8,128)(2,1)} fusion(bf16[32,448,896]{2,1,0:T(8,128)(2,1)} %bitcast.35, s32[1024]{0:T(1024)S(1)} %pad_clamp_fusion), kind=kCustom, calls=%fused_computation.1.clone | custom fusion | bytes 51380352 | tf_op jit(solution)/shard_map/jit(_take)/gather | solution.py:49
  1445.4 12.9 broadcast_select_fusion
  1458.3 0.0 copy-start.1
  1458.3 8.8 copy.20
  1467.1 0.0 copy-done.1
  (7 shorter events, 0.0 us)
Async XLA Ops:
  0.6 0.7 copy-start
  1.5 1.6 copy-start.2
  79.8 583.0 %all-to-all-start = ((bf16[32,448,896]{2,1,0:T(8,128)(2,1)}), bf16[32,448,896]{2,1,0:T(8,128)(2,1)}, u32[]{:S(2)}, u32[]{:S(2)}) async-start(bf16[32,448,896]{2,1,0:T(8,128)(2,1)} %broadcast_select_fusion.1), calls=%async_computation | async-start | bytes 51380224 | tf_op jit(solution)/shard_map/all_to_all | solution.py:31
  827.7 6.5 copy-start.3
  827.7 560.0 %all-to-all-start.1 = ((bf16[4,3584,896]{2,0,1:T(4,128)(2,1)}), bf16[4,3584,896]{2,0,1:T(4,128)(2,1)}, u32[]{:S(2)}, u32[]{:S(2)}) async-start(bf16[4,3584,896]{2,0,1:T(4,128)(2,1)} %copy.14), calls=%async_computation.1 | async-start | bytes 51380224 | tf_op jit(solution)/shard_map/all_to_all | solution.py:48
  1458.3 8.8 copy-start.1
where the time goes:
time: 1470 us
  blocking collectives  559 us (38%)
  waiting for transfers between devices  553 us (38%)
  local copies, waits for them, and re-layouts  182 us (12%)
  matrix products  87 us (6%)
  other arithmetic  70.6 us (5%)
    psum x1, blocking collectives, body(): lax.psum(jnp.sum(jnp.square(gradients.astype(jnp.float32))), ('dp', 'mp'))  559 us
    all_to_all x1, waiting for transfers between devices, body(): lax.all_to_all(finished, 'dp', split_axis=1, concat_axis=0, tiled=True)  553 us
    reshape x1, local copies, waits for them, and re-layouts, body(): second_product.astype(jnp.bfloat16).reshape(owned_count, D, BLOCK)  56.9 us
    dot_general x1, matrix products, body(): jnp.einsum('snab,snbc->snac', scaled, right_root, preferred_element_type=...  43.5 us
    dot_general x1, matrix products, body(): jnp.einsum('snab,snbc->snac', left_root, owned_blocks, preferred_element_...  43.5 us
    all_to_all x2, local copies, waits for them, and re-layouts, body(): lax.all_to_all(finished, 'dp', split_axis=1, concat_axis=0, tiled=True)  38.5 us
  transfers between devices with their start and end apart: 2, of which 1 were waited for; matrix products, arithmetic and copies ran while one was open for 1% of the time, Pallas kernels for 0%

commit v1 on v0

v1 whole, which is shorter than its diff:
```python
import functools
import math

import jax
import jax.numpy as jnp
from jax import lax
from jax.experimental import pallas as pl
from jax.experimental.pallas import tpu as pltpu
from jax.sharding import PartitionSpec as P

rms_limit = 0.25
epsilon = 1e-06
VMEM_LIMIT = 48 * 1024 * 1024


def pack_kernel(matrix_ref, column_ref, x_ref, o_ref, s_ref):
    @pl.when(pl.program_id(0) == 0)
    def _():
        s_ref[...] = jnp.zeros_like(s_ref)

    x = x_ref[0]
    o_ref[0] = x
    wide = x.astype(jnp.float32)
    s_ref[...] += jnp.sum((wide * wide).reshape(-1, 8, wide.shape[-1]), axis=0)


def pack(gradients, matrix_of, column_of, block):
    count = matrix_of.shape[0]
    rows = gradients.shape[1]
    spec = pltpu.PrefetchScalarGridSpec(
        num_scalar_prefetch=2,
        grid=(count,),
        in_specs=[pl.BlockSpec((1, rows, block), lambda i, m, c: (m[i], 0, c[i]))],
        out_specs=[
            pl.BlockSpec((1, rows, block), lambda i, m, c: (i, 0, 0)),
            pl.BlockSpec((8, block), lambda i, m, c: (0, 0)),
        ],
    )
    size = count * rows * block
    return pl.pallas_call(
        pack_kernel,
        grid_spec=spec,
        out_shape=[
            jax.ShapeDtypeStruct((count, rows, block), gradients.dtype),
            jax.ShapeDtypeStruct((8, block), jnp.float32),
        ],
        cost_estimate=pl.CostEstimate(
            flops=2 * size, bytes_accessed=4 * size, transcendentals=0
        ),
    )(matrix_of, column_of, gradients)


def product_kernel(clip_ref, x_ref, l_ref, r_ref, o_ref):
    block = l_ref.shape[-1]
    x = x_ref[...].reshape(block, block)
    first = jnp.dot(l_ref[0, 0, 0], x, preferred_element_type=jnp.float32)
    scaled = (clip_ref[0] * first).astype(jnp.bfloat16)
    second = jnp.dot(scaled, r_ref[0, 0, 0], preferred_element_type=jnp.float32)
    o_ref[...] = second.astype(o_ref.dtype).reshape(o_ref.shape)


def products(clip, received, left_roots, right_roots, first_slot):
    peers, slots, rows, block = received.shape
    row_blocks = left_roots.shape[2]
    per_block = block // rows
    root_spec = pl.BlockSpec(
        (1, 1, 1, block, block), lambda s, r: (first_slot + s, 0, r, 0, 0)
    )
    block_spec = pl.BlockSpec((per_block, 1, rows, block), lambda s, r: (r, s, 0, 0))
    count = slots * row_blocks
    return pl.pallas_call(
        product_kernel,
        grid=(slots, row_blocks),
        in_specs=[
            pl.BlockSpec(memory_space=pltpu.SMEM),
            block_spec,
            root_spec,
            root_spec,
        ],
        out_specs=block_spec,
        out_shape=jax.ShapeDtypeStruct(received.shape, received.dtype),
        compiler_params=pltpu.CompilerParams(vmem_limit_bytes=VMEM_LIMIT),
        cost_estimate=pl.CostEstimate(
            flops=4 * count * block**3,
            bytes_accessed=8 * count * block**2,
            transcendentals=0,
        ),
    )(clip, received, left_roots, right_roots)


def unpack_kernel(matrix_ref, column_ref, x_ref, *refs):
    refs[-1][0] = x_ref[0]


def unpack(returned, matrix_of, column_of, shape, partial):
    count, rows, block = returned.shape
    in_specs = [pl.BlockSpec((1, rows, block), lambda i, m, c: (i, 0, 0))]
    operands = [matrix_of, column_of, returned]
    aliases = {}
    if partial is not None:
        in_specs.append(pl.BlockSpec(memory_space=pl.ANY))
        operands.append(partial)
        aliases = {3: 0}
    spec = pltpu.PrefetchScalarGridSpec(
        num_scalar_prefetch=2,
        grid=(count,),
        in_specs=in_specs,
        out_specs=pl.BlockSpec((1, rows, block), lambda i, m, c: (m[i], 0, c[i])),
    )
    size = count * rows * block
    return pl.pallas_call(
        unpack_kernel,
        grid_spec=spec,
        out_shape=jax.ShapeDtypeStruct(shape, returned.dtype),
        input_output_aliases=aliases,
        cost_estimate=pl.CostEstimate(
            flops=0, bytes_accessed=4 * size, transcendentals=0
        ),
    )(*operands)


def body(peers, total, gradients, column_slot, left_roots, right_roots):
    matrices, rows, width = gradients.shape
    owned, block = left_roots.shape[0], left_roots.shape[-1]
    local_cols = width // block
    chunks = 2 if owned % 2 == 0 else 1
    per = owned // chunks
    slot_count = matrices * local_cols
    mp_index = lax.axis_index("mp")
    my_slots = lax.dynamic_slice_in_dim(
        column_slot, mp_index * local_cols, local_cols, 1
    ).reshape(slot_count)
    ids = jnp.arange(slot_count, dtype=jnp.int32)
    order = jnp.sum(jnp.where(my_slots[None, :] == ids[:, None], ids[None, :], 0), axis=1)
    order = order.astype(jnp.int32).reshape(peers, chunks, per)
    matrix_of = [(order[:, k] // local_cols).reshape(-1) for k in range(chunks)]
    column_of = [(order[:, k] % local_cols).reshape(-1) for k in range(chunks)]

    packed, sums = [], []
    for k in range(chunks):
        chunk, partial = pack(gradients, matrix_of[k], column_of[k], block)
        packed.append(chunk)
        sums.append(partial)
    square_sum = lax.psum(jnp.sum(functools.reduce(jnp.add, sums)), ("dp", "mp"))
    clip_scale = jnp.minimum(
        jnp.float32(1.0), rms_limit / jnp.sqrt(square_sum / total + epsilon)
    )
    clip_scale, *packed = lax.optimization_barrier((clip_scale, *packed))
    clip = clip_scale.reshape(1)
    exchange = functools.partial(
        lax.all_to_all, axis_name="dp", split_axis=0, concat_axis=0, tiled=True
    )
    received = [exchange(c) for c in packed]
    returned = []
    for k in range(chunks):
        grid = received[k].reshape(peers, per, rows, block)
        finished = products(clip, grid, left_roots, right_roots, k * per)
        returned.append(exchange(finished.reshape(peers * per, rows, block)))
    update = None
    for k in range(chunks):
        update = unpack(returned[k], matrix_of[k], column_of[k], gradients.shape, update)
    return (update, clip_scale)


def solution(mesh):
    def run(gradients, column_slot, left_roots, right_roots):
        mapped = jax.shard_map(
            functools.partial(body, mesh.shape["dp"], math.prod(gradients.shape)),
            mesh=mesh,
            in_specs=(
                P(None, "dp", "mp"),
                P(),
                P("dp", "mp", None, None, None),
                P("dp", "mp", None, None, None),
            ),
            out_specs=(P(None, "dp", "mp"), P()),
            check_vma=False,
        )
        return mapped(gradients, column_slot, left_roots, right_roots)

    return run
```

time: 1470 us -> 1230 us (0.84)
  blocking collectives: 559 us -> 328 us
  waiting for transfers between devices: 553 us -> 747 us
  local copies, waits for them, and re-layouts: 182 us -> 1.13 us
  Pallas kernels: 0 us -> 134 us
  matrix products: 87 us -> 0 us
  other arithmetic: 70.6 us -> 2.55 us
    psum x1, blocking collectives: 559 us -> 42.2 us  [body(): lax.psum(jnp.sum(functools.reduce(jnp.add, sums)), ('dp', 'mp'))]
    all_to_all x0 -> x1, blocking collectives: none -> 286 us  [body(): received = [exchange(c) for c in packed]]
    all_to_all x2 -> x3, waiting for transfers between devices: 553 us -> 747 us  [the longest x2 504 us: body(): returned.append(exchange(finished.reshape(peers * per, rows, block)))]
    pallas_call x0 -> x6, Pallas kernels: none -> 134 us  [the longest x2 69.4 us: products(): pl.pallas_call(product_kernel, grid=(slots, row_blocks), in_specs=[pl.Blo...]
    dot_general x2 -> x0, matrix products: 87 us -> none  [the longest x1 43.5 us: body(): jnp.einsum('snab,snbc->snac', scaled, right_root, preferred_element_type=...]
    reshape x3 -> x1, local copies, waits for them, and re-layouts: 65.8 us -> 0.1 us  [body(): order = order.astype(jnp.int32).reshape(peers, chunks, per)]
    all_to_all x3 -> x0, local copies, waits for them, and re-layouts: 59.5 us -> none  [the longest x2 38.5 us: body(): lax.all_to_all(finished, 'dp', split_axis=1, concat_axis=0, tiled=True)]
    gather x2 -> x0, local copies, waits for them, and re-layouts: 38.1 us -> none  [the longest x1 19.2 us: body(): restored = jnp.take(returned, my_slots, axis=0)]
  transfers between devices with their start and end apart: 2 -> 3, of which waited for: 1 -> 3; matrix products, arithmetic and copies ran while one was open for 1% -> 0% of each run, Pallas kernels for 0% -> 7%
where the time goes in v1:
time: 1230 us
  waiting for transfers between devices  747 us (61%)
  blocking collectives  328 us (27%)
  Pallas kernels  134 us (11%)
  starting transfers between devices  16.1 us (1%)
    all_to_all x2, waiting for transfers between devices, body(): returned.append(exchange(finished.reshape(peers * per, rows, block)))  504 us
    all_to_all x1, blocking collectives, body(): received = [exchange(c) for c in packed]  286 us
    all_to_all x1, waiting for transfers between devices, body(): received = [exchange(c) for c in packed]  243 us
    pallas_call x2, Pallas kernels, products(): pl.pallas_call(product_kernel, grid=(slots, row_blocks), in_specs=[pl.Blo...  69.4 us
    psum x1, blocking collectives, body(): lax.psum(jnp.sum(functools.reduce(jnp.add, sums)), ('dp', 'mp'))  42.2 us
    pallas_call x2, Pallas kernels, pack(): pl.pallas_call(pack_kernel, grid_spec=spec, out_shape=[jax.ShapeDtypeStru...  32.1 us
    pallas_call x2, Pallas kernels, unpack(): pl.pallas_call(unpack_kernel, grid_spec=spec, out_shape=jax.ShapeDtypeStr...  32.1 us
  transfers between devices with their start and end apart: 3, of which 3 were waited for; matrix products, arithmetic and copies ran while one was open for 0% of the time, Pallas kernels for 7%

profile of v1, /device:TPU:0, one launch (start us, length us, event | category | flops | bytes accessed | tf_op | source)
XLA Modules:
  0.0 1230.7 jit_solution(18430660530258803969)
XLA Ops:
  0.6 0.0 copy-start
  0.7 0.7 copy-done
  1.3 0.1 constant_dynamic-slice_fusion
  1.4 0.1 eq.18
  1.5 0.1 select_reduce_fusion
  1.6 0.1 reshape.31
  1.7 0.1 squeeze.9
  1.8 0.1 squeeze.8
  1.9 0.5 and_select_fusion.2
  2.4 0.5 and_select_fusion
  3.0 16.0 %shard_map.59 = (bf16[16,448,896]{2,1,0:T(8,128)(2,1)}, f32[8,896]{1,0:T(8,128)}) custom-call(s32[16]{0:T(128)} %get-tuple-element.19.matrix_ref, s32[16]{0:T(128)} %get-tuple-element.18.column_ref, bf16[8,448,3584]{2,1,0:T(8,128)(2,1)} %x_ref.3), custom_call_target="tpu_custom_call" | custom-call | flops 12845056 | bytes 25690112 | tf_op jit(solution)/shard_map/pallas_call | solution.py:40
  18.9 0.0 copy-start.2
  18.9 16.2 %shard_map.60 = (bf16[16,448,896]{2,1,0:T(8,128)(2,1)}, f32[8,896]{1,0:T(8,128)}) custom-call(s32[16]{0:T(128)} %get-tuple-element.21.matrix_ref, s32[16]{0:T(128)} %get-tuple-element.20.column_ref, bf16[8,448,3584]{2,1,0:T(8,128)(2,1)} %x_ref.3), custom_call_target="tpu_custom_call" | custom-call | flops 12845056 | bytes 25690112 | tf_op jit(solution)/shard_map/pallas_call | solution.py:40
  35.1 0.0 copy-done.2
  35.1 1.4 add_reduce_fusion
  36.5 42.2 %psum.7 = f32[]{:T(128)} all-reduce(f32[]{:T(128)} %add_reduce_fusion), channel_id=1, replica_groups=mesh['dp'=8,'mp'=4] {'dp','mp'}, use_global_device_ids=true, to_apply=%region_2.3 | all-reduce | flops 1 | bytes 8 | tf_op jit(solution)/shard_map/psum | solution.py:144
  79.3 285.5 %all_to_all.20 = bf16[16,448,896]{2,1,0:T(8,128)(2,1)} all-to-all(bf16[16,448,896]{2,1,0:T(8,128)(2,1)} %get-tuple-element.15), channel_id=1, replica_groups=mesh['dp'=8,'mp'=4] {'dp'}, dimensions={0} | all-to-all | bytes 25690112 | tf_op jit(solution)/shard_map/all_to_all | solution.py:153
  364.9 5.4 all-to-all-start
  370.2 34.6 %shard_map.62 = bf16[8,2,448,896]{3,2,1,0:T(8,128)(2,1)} custom-call(f32[1]{0:T(128)} %bitcast.clip_ref, bf16[8,2,448,896]{3,2,1,0:T(8,128)(2,1)} %bitcast.7, bf16[4,1,4,896,896]{4,3,2,1,0:T(8,128)(2,1)} %l_ref.3, bf16[4,1,4,896,896]{4,3,2,1,0:T(8,128)(2,1)} %r_ref.3), custom_call_target="tpu_custom_call" | custom-call | flops 23018340352 | bytes 51380224 | tf_op jit(solution)/shard_map/pallas_call | solution.py:71
  404.9 243.0 %all-to-all-done = bf16[16,448,896]{2,1,0:T(8,128)(2,1)} async-done(((bf16[16,448,896]{2,1,0:T(8,128)(2,1)}), bf16[16,448,896]{2,1,0:T(8,128)(2,1)}, u32[]{:S(2)}, u32[]{:S(2)}) %all-to-all-start) | async-done | bytes 12845088 | tf_op jit(solution)/shard_map/all_to_all | solution.py:153
  647.9 5.4 all-to-all-start.3
  653.3 34.7 %shard_map.61 = bf16[8,2,448,896]{3,2,1,0:T(8,128)(2,1)} custom-call(f32[1]{0:T(128)} %bitcast.clip_ref, bf16[8,2,448,896]{3,2,1,0:T(8,128)(2,1)} %bitcast.1.x_ref, bf16[4,1,4,896,896]{4,3,2,1,0:T(8,128)(2,1)} %l_ref.3, bf16[4,1,4,896,896]{4,3,2,1,0:T(8,128)(2,1)} %r_ref.3), custom_call_target="tpu_custom_call" | custom-call | flops 23018340352 | bytes 51380224 | tf_op jit(solution)/shard_map/pallas_call | solution.py:71
  688.0 242.3 %all-to-all-done.3.x_ref = bf16[16,448,896]{2,1,0:T(8,128)(2,1)} async-done(((bf16[16,448,896]{2,1,0:T(8,128)(2,1)}), bf16[16,448,896]{2,1,0:T(8,128)(2,1)}, u32[]{:S(2)}, u32[]{:S(2)}) %all-to-all-start.3) | async-done | bytes 12845088 | tf_op jit(solution)/shard_map/all_to_all | solution.py:158
  930.4 5.4 all-to-all-start.1
  935.8 16.0 %shard_map.63.refs_0_ = bf16[8,448,3584]{2,1,0:T(8,128)(2,1)} custom-call(s32[16]{0:T(128)} %get-tuple-element.19.matrix_ref, s32[16]{0:T(128)} %get-tuple-element.18.column_ref, bf16[16,448,896]{2,1,0:T(8,128)(2,1)} %all-to-all-done.3.x_ref), custom_call_target="tpu_custom_call" | custom-call | bytes 25690112 | tf_op jit(solution)/shard_map/pallas_call | solution.py:111
  951.7 261.7 %all-to-all-done.1.x_ref = bf16[16,448,896]{2,1,0:T(8,128)(2,1)} async-done(((bf16[16,448,896]{2,1,0:T(8,128)(2,1)}), bf16[16,448,896]{2,1,0:T(8,128)(2,1)}, u32[]{:S(2)}, u32[]{:S(2)}) %all-to-all-start.1) | async-done | bytes 12845088 | tf_op jit(solution)/shard_map/all_to_all | solution.py:158
  1213.5 0.0 copy-start.1
  1213.5 16.1 %shard_map.64 = bf16[8,448,3584]{2,1,0:T(8,128)(2,1)} custom-call(s32[16]{0:T(128)} %get-tuple-element.21.matrix_ref, s32[16]{0:T(128)} %get-tuple-element.20.column_ref, bf16[16,448,896]{2,1,0:T(8,128)(2,1)} %all-to-all-done.1.x_ref, bf16[8,448,3584]{2,1,0:T(8,128)(2,1)} %shard_map.63.refs_0_), custom_call_target="tpu_custom_call", output_to_operand_aliasing={{}: (3, {})} | custom-call | bytes 25690112 | tf_op jit(solution)/shard_map/pallas_call | solution.py:111
  1229.6 0.0 copy-done.1
  (1 shorter events, 0.0 us)
Async XLA Ops:
  0.6 0.7 copy-start
  18.9 16.2 %copy-start.2 = (f32[8,896]{1,0:T(8,128)S(1)}, f32[8,896]{1,0:T(8,128)}, u32[]{:S(2)}) copy-start(f32[8,896]{1,0:T(8,128)} %get-tuple-element.9) | copy-start | bytes 86020
  364.9 283.0 %all-to-all-start = ((bf16[16,448,896]{2,1,0:T(8,128)(2,1)}), bf16[16,448,896]{2,1,0:T(8,128)(2,1)}, u32[]{:S(2)}, u32[]{:S(2)}) async-start(bf16[16,448,896]{2,1,0:T(8,128)(2,1)} %get-tuple-element.14), calls=%async_computation | async-start | bytes 25690112 | tf_op jit(solution)/shard_map/all_to_all | solution.py:153
  647.9 282.5 %all-to-all-start.3 = ((bf16[16,448,896]{2,1,0:T(8,128)(2,1)}), bf16[16,448,896]{2,1,0:T(8,128)(2,1)}, u32[]{:S(2)}, u32[]{:S(2)}) async-start(bf16[16,448,896]{2,1,0:T(8,128)(2,1)} %bitcast.6), calls=%async_computation.3 | async-start | bytes 25690112 | tf_op jit(solution)/shard_map/all_to_all | solution.py:158
  930.4 283.1 %all-to-all-start.1 = ((bf16[16,448,896]{2,1,0:T(8,128)(2,1)}), bf16[16,448,896]{2,1,0:T(8,128)(2,1)}, u32[]{:S(2)}, u32[]{:S(2)}) async-start(bf16[16,448,896]{2,1,0:T(8,128)(2,1)} %bitcast.5), calls=%async_computation.1 | async-start | bytes 25690112 | tf_op jit(solution)/shard_map/all_to_all | solution.py:158
  1213.5 16.1 %copy-start.1 = (s32[8,16]{1,0:T(8,128)S(1)}, s32[8,16]{1,0:T(8,128)}, u32[]{:S(2)}) copy-start(s32[8,16]{1,0:T(8,128)} %param.5) | copy-start | bytes 1540
